TPU v7x, 32 devices: a whole 2x2x4 slice. The times are simulated.
32 devices in a mesh: shard: 32 (over z, y, x, core).
Axes of the slice: x: 2, y: 2, z: 4, core: 2. Of those that a mesh axis runs over, the one named last changes fastest.
Arguments:
- data_t: bfloat16 [8192, 8192], P('shard'), may hold values from -0.125 to 0.125
- labels: int32 [8192], replicated, may hold values from -1 to 1, as said below
- sample_weight: float32 [8192], replicated, may hold values from 0.1 to 4
- w_start: float32 [8192], P('shard'), may hold values from -10 to 10
- alpha_start: float32 [8192], P('shard'), may hold values from 0 to 1
- visit_order: int32 [64, 128], P('shard'), may hold values from 0 to 127, each once within a row
Outputs:
- weights_out: float32 [8192], P('shard')
- alpha_final: float32 [8192], P('shard')
- objective: float32 [], replicated
Inputs may be any that keep to these rules, and one draw needn't show every extreme that they name: `labels`: each label is -1 or +1. `visit_order`: each row is a permutation of 0 to 127.
All inputs are finite; a program needn't handle non-finite values.
Results may differ from a plain program's by a relative error of at most 0.0047.
Values may be sent and summed in bfloat16 or wider, within the bound.
A program may use at most 64 MiB of HBM per device.

v0:
```python
import jax
import jax.numpy as jnp
from jax import lax
from jax.sharding import PartitionSpec as P

GROUP = 16


def sweep_rows(gram_block, label_rows, bound_rows, alpha_rows, margin_rows, visit_rows):
    gram_perm = gram_block[visit_rows][:, visit_rows]
    label_perm = label_rows[visit_rows]
    bound_perm = bound_rows[visit_rows]
    alpha_perm = alpha_rows[visit_rows]
    margin_perm = margin_rows[visit_rows]
    diag_perm = jnp.diagonal(gram_perm) + 1e-06

    def update_group(group_index, state_pair):
        alpha_now, margin_now = state_pair
        first_row = jnp.asarray(group_index * GROUP).astype(jnp.int32)
        group_alpha = lax.dynamic_slice_in_dim(alpha_now, first_row, GROUP)
        group_label = lax.dynamic_slice_in_dim(label_perm, first_row, GROUP)
        group_margin = lax.dynamic_slice_in_dim(margin_now, first_row, GROUP)
        group_diag = lax.dynamic_slice_in_dim(diag_perm, first_row, GROUP)
        group_bound = lax.dynamic_slice_in_dim(bound_perm, first_row, GROUP)
        fresh_alpha = jnp.clip(
            group_alpha + (1.0 - group_label * group_margin) / (2.0 * group_diag), 0.0, group_bound
        )
        change = fresh_alpha - group_alpha
        columns = lax.dynamic_slice_in_dim(gram_perm, first_row, GROUP, 1)
        margin_now = margin_now + 2.0 * jnp.dot(
            columns, group_label * change, precision=lax.Precision.HIGHEST
        )
        alpha_now = lax.dynamic_update_slice_in_dim(alpha_now, fresh_alpha, first_row, 0)
        return (alpha_now, margin_now)

    alpha_perm, margin_perm = lax.fori_loop(
        0, alpha_rows.shape[0] // GROUP, update_group, (alpha_perm, margin_perm)
    )
    return jnp.zeros_like(alpha_rows).at[visit_rows].set(alpha_perm)


def body(data_t, labels, sample_weight, w_start, alpha_start, visit_order):
    device_index = lax.axis_index("shard")
    devices = lax.axis_size("shard")
    local_feat = data_t.shape[0]
    samples = labels.shape[0]
    row_count = alpha_start.shape[0]
    features = local_feat * devices
    label_sign = labels.astype(jnp.float32)
    row_first = device_index * row_count
    own_signs = lax.dynamic_slice_in_dim(label_sign, row_first, row_count)
    own_bound = lax.dynamic_slice_in_dim(sample_weight, row_first, row_count)
    relaid = lax.all_to_all(data_t, "shard", split_axis=1, concat_axis=0, tiled=True)
    start_part = jnp.dot(w_start.astype(jnp.bfloat16), data_t, preferred_element_type=jnp.float32)
    start_margin = lax.psum(start_part, "shard")
    weighted = (
        sample_weight * label_sign * jnp.maximum(0.0, 1.0 - label_sign * start_margin)
    ).astype(jnp.bfloat16)
    ascent = jnp.dot(data_t, weighted, preferred_element_type=jnp.float32)
    column_sq = jnp.einsum("fs,fs->f", data_t, data_t, preferred_element_type=jnp.float32)
    scale_col = column_sq / samples + 1e-06
    stepped = w_start + ascent / (samples * scale_col)
    thresh = 1.0 / (4.0 * features * scale_col)
    primal = stepped - jnp.clip(stepped, -thresh, thresh)
    model_part = jnp.dot(primal.astype(jnp.bfloat16), data_t, preferred_element_type=jnp.float32)
    penalty_part = jnp.sum(jnp.abs(primal)) / (4.0 * features)
    own_margin = lax.psum_scatter(model_part, "shard", scatter_dimension=0, tiled=True)
    loss_part = jnp.sum(own_bound * jnp.square(jnp.maximum(0.0, 1.0 - own_signs * own_margin))) / (
        2.0 * samples
    )
    loss_total, penalty = lax.psum((loss_part, penalty_part), "shard")
    objective = loss_total + penalty
    gram_block = lax.dot_general(
        relaid, relaid, (((0,), (0,)), ((), ())), preferred_element_type=jnp.float32
    )
    block_count = visit_order.shape[0]
    visit_rows = (
        visit_order + (jnp.arange(block_count, dtype=jnp.int32) * visit_order.shape[1])[:, None]
    ).reshape(row_count)
    alpha_zero = own_bound * alpha_start
    alpha_one = sweep_rows(gram_block, own_signs, own_bound, alpha_zero, own_margin, visit_rows)
    change_one = (own_signs * (alpha_one - alpha_zero)).astype(jnp.bfloat16)
    update_part = jnp.dot(relaid, change_one, preferred_element_type=jnp.float32) * (2.0 / devices)
    update_one = lax.psum(update_part, "shard")
    second_margin = own_margin + jnp.dot(
        update_one.astype(jnp.bfloat16), relaid, preferred_element_type=jnp.float32
    )
    alpha_two = sweep_rows(gram_block, own_signs, own_bound, alpha_one, second_margin, visit_rows)
    change_two = (own_signs * (alpha_two - alpha_one)).astype(jnp.bfloat16)
    second_part = jnp.dot(relaid, change_two, preferred_element_type=jnp.float32) * (2.0 / devices)
    feat_first = device_index * local_feat
    update_two = lax.psum(second_part, "shard")
    own_two = lax.dynamic_slice_in_dim(update_two, feat_first, local_feat)
    own_one = lax.dynamic_slice_in_dim(update_one, feat_first, local_feat)
    return (primal + own_one + own_two, alpha_two, objective)


def solution(mesh):
    placed = (P("shard", None), P(), P(), P("shard"), P("shard"), P("shard", None))
    return jax.shard_map(
        body, mesh=mesh, in_specs=placed, out_specs=(P("shard"), P("shard"), P()), check_vma=False
    )
```

profile of v0, /device:TPU:14, one launch (start us, length us, event | category | flops | bytes accessed | tf_op | source)
XLA Modules:
  0.0 315.5 jit_solution(12440864550533348112)
XLA Ops:
  0.6 6.4 %copy.19 = bf16[256,8192]{0,1:T(8,128)(2,1)} copy(bf16[256,8192]{1,0:T(8,128)(2,1)} %param.10) | data formatting | bytes 8388608 | tf_op args[0]
  7.0 6.4 %copy.20 = bf16[256,32,256]{2,0,1:T(8,128)(2,1)} copy(bf16[256,32,256]{0,2,1:T(8,128)(2,1)} %bitcast.48) | data formatting | bytes 8388608 | tf_op jit(solution)/shard_map/all_to_all | solution.py:53
  13.4 6.0 %all-to-all-start = ((bf16[256,32,256]{2,0,1:T(8,128)(2,1)}), bf16[256,32,256]{2,0,1:T(8,128)(2,1)}, u32[]{:S(2)}, u32[]{:S(2)}) async-start(bf16[256,32,256]{2,0,1:T(8,128)(2,1)} %copy.20), calls=%async_computation | async-start | bytes 8388608 | tf_op jit(solution)/shard_map/all_to_all | solution.py:53
  19.5 2.8 fusion.28
  22.4 109.1 %psum.35 = f32[8192]{0:T(1024)S(1)} all-reduce(f32[8192]{0:T(1024)S(1)} %bitcast.53), channel_id=1, replica_groups=mesh['shard'=32] {'shard'}, use_global_device_ids=true, to_apply=%region_0.0 | all-reduce | flops 8192 | bytes 65536 | tf_op jit(solution)/shard_map/psum | solution.py:55
  131.5 3.5 %fusion.29 = f32[1,256]{1,0:T(1,128)S(1)} fusion(bf16[8192,1]{0,1:T(2,128)(2,1)S(1)} %reshape.137, bf16[256,8192]{1,0:T(8,128)(2,1)} %param.10), kind=kOutput, calls=%fused_computation.58 | convolution fusion | flops 4194304 | bytes 4211712 | tf_op jit(solution)/shard_map/dot_general | solution.py:59
  135.1 0.9 fusion.16
  136.0 0.6 abs_reduce_fusion
  136.6 2.8 fusion.30
  139.5 42.1 %all-reduce = f32[8192]{0:T(1024)S(1)} all-reduce(f32[8192]{0:T(1024)S(1)} %bitcast.54), channel_id=2, replica_groups=mesh['shard'=32] {'shard'}, use_global_device_ids=true, to_apply=%region_1.2.clone | all-reduce | flops 8192 | bytes 65536
  181.6 0.7 multiply_reduce_fusion
  182.3 1.9 gather_fusion.3
  184.3 1.9 gather_fusion.2
  186.3 1.9 gather_fusion
  188.2 1.9 gather_fusion.1
  191.5 4.7 %fusion.19 = f32[256,256]{1,0:T(8,128)S(1)} fusion(bf16[256,32,256]{2,0,1:T(8,128)(2,1)} %all-to-all-done), kind=kOutput, calls=%fused_computation.35 | convolution fusion | flops 1073741824 | bytes 4456448 | tf_op jit(solution)/shard_map/dot_general | solution.py:73
  196.2 1.0 gather_fusion.4
  197.3 1.0 gather_fusion.5
  198.5 2.4 gather_fusion.6
  200.8 8.5 %while.30 = (s32[]{:T(128)}, f32[256]{0:T(256)S(1)}, f32[256]{0:T(256)S(1)}, f32[256]{0:T(256)S(1)}, f32[256]{0:T(256)S(1)}, /*index=5*/f32[256]{0:T(256)S(1)}, ...) while((s32[]{:T(128)}, f32[256]{0:T(256)S(1)}, f32[256]{0:T(256)S(1)}, ...), condition=%wide.region_3.4_spmd, body=%wide.region_2.3_spmd.sunk | while | flops 49814 | bytes 145567 | solution.py:36
  201.1 0.2 fusion.57
  209.3 1.4 scatter_custom_fusion
  210.7 1.9 gather_fusion.7
  212.7 3.4 %fusion.31 = f32[1,8192]{1,0:T(1,128)S(1)} fusion(bf16[256,1]{0,1:T(2,128)(2,1)S(1)} %reshape.144, bf16[8192,256]{1,0:T(8,128)(2,1)} %bitcast.14), kind=kOutput, calls=%fused_computation.60 | convolution fusion | flops 4194304 | bytes 4227584 | tf_op jit(solution)/shard_map/dot_general | solution.py:83
  216.1 38.4 %psum.36 = f32[8192]{0:T(1024)S(1)} all-reduce(f32[8192]{0:T(1024)S(1)} %broadcast_multiply_fusion.1), channel_id=1, replica_groups=mesh['shard'=32] {'shard'}, use_global_device_ids=true, to_apply=%region_5.6 | all-reduce | flops 8192 | bytes 65536 | tf_op jit(solution)/shard_map/psum | solution.py:84
  254.5 2.8 fusion.32
  257.4 2.0 gather_fusion.8
  259.3 8.5 %while.31 = (s32[]{:T(128)}, f32[256]{0:T(256)S(1)}, f32[256]{0:T(256)S(1)}, f32[256]{0:T(256)S(1)}, f32[256]{0:T(256)S(1)}, /*index=5*/f32[256]{0:T(256)S(1)}, ...) while((s32[]{:T(128)}, f32[256]{0:T(256)S(1)}, f32[256]{0:T(256)S(1)}, ...), condition=%wide.region_7.8_spmd, body=%wide.region_6.7_spmd.sunk | while | flops 49814 | bytes 145567 | solution.py:36
  267.8 1.4 scatter_custom_fusion.1
  269.2 3.4 %fusion.33 = f32[1,8192]{1,0:T(1,128)S(1)} fusion(bf16[256,1]{0,1:T(2,128)(2,1)S(1)} %reshape.148, bf16[8192,256]{1,0:T(8,128)(2,1)} %bitcast.14), kind=kOutput, calls=%fused_computation.62 | convolution fusion | flops 4194304 | bytes 4227584 | tf_op jit(solution)/shard_map/dot_general | solution.py:90
  272.6 42.2 %all-reduce.1 = (f32[8192]{0:T(1024)S(1)}, f32[]{:T(128)}) all-reduce(f32[8192]{0:T(1024)S(1)} %broadcast_multiply_fusion, f32[]{:T(128)S(6)} %add.173), channel_id=1, replica_groups=mesh['shard'=32] {'shard'}, use_global_device_ids=true, to_apply=%region_9.10 | all-reduce | flops 8193 | bytes 65544 | tf_op jit(solution)/shard_map/psum | solution.py:92
  314.8 0.6 dynamic-slice_add_fusion
  (199 shorter events, 15.8 us)
Async XLA Ops:
  13.4 6.1 %copy-start.6 = (f32[256]{0:T(256)S(1)}, f32[256]{0:T(256)}, u32[]{:S(2)}) copy-start(f32[256]{0:T(256)} %param.13) | copy-start | bytes 3076
  13.4 6.1 %copy-start.1 = (s32[8192]{0:T(1024)S(1)}, s32[8192]{0:T(1024)}, u32[]{:S(2)}) copy-start(s32[8192]{0:T(1024)} %param.11) | copy-start | bytes 98308
  13.4 178.0 %all-to-all-start = ((bf16[256,32,256]{2,0,1:T(8,128)(2,1)}), bf16[256,32,256]{2,0,1:T(8,128)(2,1)}, u32[]{:S(2)}, u32[]{:S(2)}) async-start(bf16[256,32,256]{2,0,1:T(8,128)(2,1)} %copy.20), calls=%async_computation | async-start | bytes 8388608 | tf_op jit(solution)/shard_map/all_to_all | solution.py:53
  19.5 112.0 %copy-start.2 = (f32[8192]{0:T(1024)S(1)}, f32[8192]{0:T(1024)}, u32[]{:S(2)}) copy-start(f32[8192]{0:T(1024)} %param.12) | copy-start | bytes 98308
  131.5 3.6 %copy-start = (bf16[256,8192]{1,0:T(8,128)(2,1)S(1)}, bf16[256,8192]{1,0:T(8,128)(2,1)}, u32[]{:S(2)}) copy-start(bf16[256,8192]{1,0:T(8,128)(2,1)} %param.10) | copy-start | bytes 12582916
  135.1 47.2 %copy-start.5 = (s32[2,128]{1,0:T(2,128)S(1)}, s32[2,128]{1,0:T(2,128)}, u32[]{:S(2)}) copy-start(s32[2,128]{1,0:T(2,128)} %param.15) | copy-start | bytes 3076
  136.0 50.2 %copy-start.3 = (f32[256]{0:T(256)S(1)}, f32[256]{0:T(256)}, u32[]{:S(2)}) copy-start(f32[256]{0:T(256)} %param.14) | copy-start | bytes 3076
  269.2 46.3 %copy-start.4 = (f32[256]{0:T(256)}, f32[256]{0:T(256)S(1)}, u32[]{:S(2)}) copy-start(f32[256]{0:T(256)S(1)} %scatter_custom_fusion.1) | copy-start | bytes 3076
where the time goes:
time: 316 us; the launch traced here: 315 us
  blocking collectives  232 us (73%)
  local copies, waits for them, and re-layouts  32.1 us (10%)
  matrix products  31.5 us (10%)
  other arithmetic  10.4 us (3%)
  starting transfers between devices  6.02 us (2%)
    psum x1, blocking collectives, body(): start_margin = lax.psum(start_part, 'shard')  109 us
    psum x1, blocking collectives, body(): update_two = lax.psum(second_part, 'shard')  42.2 us
    unnamed x1, blocking collectives  42.1 us
    psum x1, blocking collectives, body(): update_one = lax.psum(update_part, 'shard')  38.4 us
    dot_general x32, matrix products, update_group(): jnp.dot(columns, group_label * change, precision=lax.Precision.HIGHEST)  7.97 us
    unnamed x15, local copies, waits for them, and re-layouts  6.44 us
    all_to_all x1, local copies, waits for them, and re-layouts, body(): lax.all_to_all(data_t, 'shard', split_axis=1, concat_axis=0, tiled=True)  6.41 us
  transfers between devices with their start and end apart: 1, of which 0 were waited for; matrix products, arithmetic and copies ran while one was open for 6% of the time, Pallas kernels for 0%

commit v1 on v0

--- a/solution.py
+++ b/solution.py
@@ -52,7 +52,13 @@
     own_bound = lax.dynamic_slice_in_dim(sample_weight, row_first, row_count)
     relaid = lax.all_to_all(data_t, "shard", split_axis=1, concat_axis=0, tiled=True)
     start_part = jnp.dot(w_start.astype(jnp.bfloat16), data_t, preferred_element_type=jnp.float32)
-    start_margin = lax.psum(start_part, "shard")
+    count = lax.axis_size("shard")
+    start_margin, stride = (start_part, 1)
+    while stride < count:
+        start_margin = start_margin + lax.ppermute(
+            start_margin, "shard", [(i, i ^ stride) for i in range(count)]
+        )
+        stride = 2 * stride
     weighted = (
         sample_weight * label_sign * jnp.maximum(0.0, 1.0 - label_sign * start_margin)
     ).astype(jnp.bfloat16)

time: 316 us -> 294 us (0.930)
  blocking collectives: 232 us -> 122 us
  waiting for transfers between devices: 0.01 us -> 80.8 us
  starting transfers between devices: 6.02 us -> 13.3 us
    psum x1 -> x0, blocking collectives: 109 us -> none  [body(): start_margin = lax.psum(start_part, 'shard')]
    ppermute x0 -> x5, waiting for transfers between devices: none -> 80.8 us  [body(): lax.ppermute(start_margin, 'shard', [(i, i ^ stride) for i in range(count)])]
    ppermute x0 -> x5, starting transfers between devices: none -> 7.26 us  [body(): lax.ppermute(start_margin, 'shard', [(i, i ^ stride) for i in range(count)])]
    unnamed x15 -> x17, local copies, waits for them, and re-layouts: 6.44 us -> 6.7 us
  transfers between devices with their start and end apart: 1 -> 6, of which waited for: 0 -> 4; matrix products, arithmetic and copies ran while one was open for 6% -> 6% of each run, Pallas kernels for 0% -> 0%
where the time goes in v1:
time: 294 us; the launch traced here: 292 us
  blocking collectives  122 us (41%)
  waiting for transfers between devices  80.8 us (27%)
  local copies, waits for them, and re-layouts  32.4 us (11%)
  matrix products  29.3 us (10%)
  starting transfers between devices  13.3 us (5%)
  other arithmetic  10.4 us (4%)
    ppermute x5, waiting for transfers between devices, body(): lax.ppermute(start_margin, 'shard', [(i, i ^ stride) for i in range(count)])  80.8 us
    unnamed x1, blocking collectives  41.4 us
    psum x1, blocking collectives, body(): update_two = lax.psum(second_part, 'shard')  40.7 us
    psum x1, blocking collectives, body(): update_one = lax.psum(update_part, 'shard')  39.9 us
    dot_general x32, matrix products, update_group(): jnp.dot(columns, group_label * change, precision=lax.Precision.HIGHEST)  7.97 us
    ppermute x5, starting transfers between devices, body(): lax.ppermute(start_margin, 'shard', [(i, i ^ stride) for i in range(count)])  7.26 us
    unnamed x17, local copies, waits for them, and re-layouts  6.7 us
    all_to_all x1, local copies, waits for them, and re-layouts, body(): lax.all_to_all(data_t, 'shard', split_axis=1, concat_axis=0, tiled=True)  6.48 us
  transfers between devices with their start and end apart: 6, of which 4 were waited for; matrix products, arithmetic and copies ran while one was open for 6% of the time, Pallas kernels for 0%

profile of v1, /device:TPU:14, one launch (start us, length us, event | category | flops | bytes accessed | tf_op | source)
XLA Modules:
  0.0 291.9 jit_solution(1930721526632924787)
XLA Ops:
  0.6 6.4 %copy.19 = bf16[256,8192]{0,1:T(8,128)(2,1)} copy(bf16[256,8192]{1,0:T(8,128)(2,1)} %param.10) | data formatting | bytes 8388608 | tf_op args[0]
  7.0 6.5 %copy.20 = bf16[256,32,256]{2,0,1:T(8,128)(2,1)} copy(bf16[256,32,256]{0,2,1:T(8,128)(2,1)} %bitcast.48) | data formatting | bytes 8388608 | tf_op jit(solution)/shard_map/all_to_all | solution.py:53
  13.5 6.0 %all-to-all-start = ((bf16[256,32,256]{2,0,1:T(8,128)(2,1)}), bf16[256,32,256]{2,0,1:T(8,128)(2,1)}, u32[]{:S(2)}, u32[]{:S(2)}) async-start(bf16[256,32,256]{2,0,1:T(8,128)(2,1)} %copy.20), calls=%async_computation | async-start | bytes 8388608 | tf_op jit(solution)/shard_map/all_to_all | solution.py:53
  19.6 3.0 %fusion.28 = f32[1,8192]{1,0:T(1,128)S(1)} fusion(bf16[256,1]{0,1:T(2,128)(2,1)S(1)} %reshape.135, bf16[256,8192]{1,0:T(8,128)(2,1)} %param.10), kind=kOutput, calls=%fused_computation.57 | convolution fusion | flops 4194304 | bytes 4227584 | tf_op jit(solution)/shard_map/dot_general | solution.py:54
  23.0 0.9 fusion.16
  24.6 20.9 %collective-permute-done.1 = f32[8192]{0:T(1024)S(1)} collective-permute-done((f32[8192]{0:T(1024)S(1)}, f32[8192]{0:T(1024)S(1)}, u32[]{:S(2)}, u32[]{:S(2)}) %collective-permute-start.1) | collective-permute-done | bytes 32800 | tf_op jit(solution)/shard_map/ppermute | solution.py:58
  45.5 3.9 %collective-permute-done.2 = f32[8192]{0:T(1024)S(1)} collective-permute-done((f32[8192]{0:T(1024)S(1)}, f32[8192]{0:T(1024)S(1)}, u32[]{:S(2)}, u32[]{:S(2)}) %collective-permute-start.2) | collective-permute-done | bytes 32800 | tf_op jit(solution)/shard_map/ppermute | solution.py:58
  49.4 5.6 %collective-permute-start.3 = (f32[8192]{0:T(1024)S(1)}, f32[8192]{0:T(1024)S(1)}, u32[]{:S(2)}, u32[]{:S(2)}) collective-permute-start(f32[8192]{0:T(1024)S(1)} %add.178), channel_id=1, source_target_pairs={{0,8},{1,9},{2,10},{3,11},{4,12},{5,13},{6,14},{7,15},{8,0},{9,1},... | collective-permute-start | bytes 98312 | tf_op jit(solution)/shard_map/ppermute | solution.py:58
  55.1 35.2 %collective-permute-done.3 = f32[8192]{0:T(1024)S(1)} collective-permute-done((f32[8192]{0:T(1024)S(1)}, f32[8192]{0:T(1024)S(1)}, u32[]{:S(2)}, u32[]{:S(2)}) %collective-permute-start.3) | collective-permute-done | bytes 32800 | tf_op jit(solution)/shard_map/ppermute | solution.py:58
  90.3 0.9 collective-permute-start.4
  91.2 20.8 %collective-permute-done.4 = f32[8192]{0:T(1024)S(1)} collective-permute-done((f32[8192]{0:T(1024)S(1)}, f32[8192]{0:T(1024)S(1)}, u32[]{:S(2)}, u32[]{:S(2)}) %collective-permute-start.4) | collective-permute-done | bytes 32800 | tf_op jit(solution)/shard_map/ppermute | solution.py:58
  112.0 3.4 %fusion.29 = f32[1,256]{1,0:T(1,128)S(1)} fusion(bf16[8192,1]{0,1:T(2,128)(2,1)S(1)} %reshape.137, bf16[256,8192]{1,0:T(8,128)(2,1)} %param.10), kind=kOutput, calls=%fused_computation.58 | convolution fusion | flops 4194304 | bytes 4211712 | tf_op jit(solution)/shard_map/dot_general | solution.py:65
  116.7 41.4 %all-reduce = f32[8192]{0:T(1024)S(1)} all-reduce(f32[8192]{0:T(1024)S(1)} %bitcast.55), channel_id=2, replica_groups=mesh['shard'=32] {'shard'}, use_global_device_ids=true, to_apply=%region_0.1.clone | all-reduce | flops 8192 | bytes 65536
  158.8 1.9 gather_fusion.3
  160.7 1.9 gather_fusion.2
  162.7 1.9 gather_fusion
  164.7 1.9 gather_fusion.1
  167.9 4.7 %fusion.19 = f32[256,256]{1,0:T(8,128)S(1)} fusion(bf16[256,32,256]{2,0,1:T(8,128)(2,1)} %all-to-all-done), kind=kOutput, calls=%fused_computation.35 | convolution fusion | flops 1073741824 | bytes 4456448 | tf_op jit(solution)/shard_map/dot_general | solution.py:79
  172.7 1.0 gather_fusion.4
  173.8 1.0 gather_fusion.5
  174.9 2.4 gather_fusion.6
  177.3 8.5 %while.30 = (s32[]{:T(128)}, f32[256]{0:T(256)S(1)}, f32[256]{0:T(256)S(1)}, f32[256]{0:T(256)S(1)}, f32[256]{0:T(256)S(1)}, /*index=5*/f32[256]{0:T(256)S(1)}, ...) while((s32[]{:T(128)}, f32[256]{0:T(256)S(1)}, f32[256]{0:T(256)S(1)}, ...), condition=%wide.region_2.3_spmd, body=%wide.region_1.2_spmd.sunk | while | flops 49814 | bytes 145567 | solution.py:36
  185.8 1.4 scatter_custom_fusion
  187.2 1.9 gather_fusion.7
  189.2 3.4 %fusion.31 = f32[1,8192]{1,0:T(1,128)S(1)} fusion(bf16[256,1]{0,1:T(2,128)(2,1)S(1)} %reshape.144, bf16[8192,256]{1,0:T(8,128)(2,1)} %bitcast.14), kind=kOutput, calls=%fused_computation.60 | convolution fusion | flops 4194304 | bytes 4227584 | tf_op jit(solution)/shard_map/dot_general | solution.py:89
  192.5 39.9 %psum.28 = f32[8192]{0:T(1024)S(1)} all-reduce(f32[8192]{0:T(1024)S(1)} %broadcast_multiply_fusion.1), channel_id=1, replica_groups=mesh['shard'=32] {'shard'}, use_global_device_ids=true, to_apply=%region_4.5 | all-reduce | flops 8192 | bytes 65536 | tf_op jit(solution)/shard_map/psum | solution.py:90
  232.5 2.8 fusion.32
  235.3 2.0 gather_fusion.8
  237.3 8.5 %while.31 = (s32[]{:T(128)}, f32[256]{0:T(256)S(1)}, f32[256]{0:T(256)S(1)}, f32[256]{0:T(256)S(1)}, f32[256]{0:T(256)S(1)}, /*index=5*/f32[256]{0:T(256)S(1)}, ...) while((s32[]{:T(128)}, f32[256]{0:T(256)S(1)}, f32[256]{0:T(256)S(1)}, ...), condition=%wide.region_6.7_spmd, body=%wide.region_5.6_spmd.sunk | while | flops 49814 | bytes 145567 | solution.py:36
  245.8 1.4 scatter_custom_fusion.1
  247.2 3.4 %fusion.33 = f32[1,8192]{1,0:T(1,128)S(1)} fusion(bf16[256,1]{0,1:T(2,128)(2,1)S(1)} %reshape.148, bf16[8192,256]{1,0:T(8,128)(2,1)} %bitcast.14), kind=kOutput, calls=%fused_computation.62 | convolution fusion | flops 4194304 | bytes 4227584 | tf_op jit(solution)/shard_map/dot_general | solution.py:96
  250.6 40.7 %all-reduce.1 = (f32[8192]{0:T(1024)S(1)}, f32[]{:T(128)}) all-reduce(f32[8192]{0:T(1024)S(1)} %broadcast_multiply_fusion, f32[]{:T(128)S(6)} %add.191), channel_id=1, replica_groups=mesh['shard'=32] {'shard'}, use_global_device_ids=true, to_apply=%region_8.9 | all-reduce | flops 8193 | bytes 65544 | tf_op jit(solution)/shard_map/psum | solution.py:98
  (214 shorter events, 19.7 us)
Async XLA Ops:
  13.5 6.0 %copy-start.7 = (f32[256]{0:T(256)S(1)}, f32[256]{0:T(256)}, u32[]{:S(2)}) copy-start(f32[256]{0:T(256)} %param.13) | copy-start | bytes 3076
  13.5 154.4 %all-to-all-start = ((bf16[256,32,256]{2,0,1:T(8,128)(2,1)}), bf16[256,32,256]{2,0,1:T(8,128)(2,1)}, u32[]{:S(2)}, u32[]{:S(2)}) async-start(bf16[256,32,256]{2,0,1:T(8,128)(2,1)} %copy.20), calls=%async_computation | async-start | bytes 8388608 | tf_op jit(solution)/shard_map/all_to_all | solution.py:53
  19.5 3.5 %copy-start = (bf16[256,8192]{1,0:T(8,128)(2,1)S(1)}, bf16[256,8192]{1,0:T(8,128)(2,1)}, u32[]{:S(2)}) copy-start(bf16[256,8192]{1,0:T(8,128)(2,1)} %param.10) | copy-start | bytes 12582916
  19.6 5.0 %copy-start.6 = (s32[2,128]{1,0:T(2,128)S(1)}, s32[2,128]{1,0:T(2,128)}, u32[]{:S(2)}) copy-start(s32[2,128]{1,0:T(2,128)} %param.15) | copy-start | bytes 3076
  19.6 71.6 %copy-start.2 = (s32[8192]{0:T(1024)S(1)}, s32[8192]{0:T(1024)}, u32[]{:S(2)}) copy-start(s32[8192]{0:T(1024)} %param.11) | copy-start | bytes 98308
  19.6 92.4 %copy-start.3 = (f32[8192]{0:T(1024)S(1)}, f32[8192]{0:T(1024)}, u32[]{:S(2)}) copy-start(f32[8192]{0:T(1024)} %param.12) | copy-start | bytes 98308
  22.6 1.3 collective-permute-start
  23.9 21.6 %collective-permute-start.1 = (f32[8192]{0:T(1024)S(1)}, f32[8192]{0:T(1024)S(1)}, u32[]{:S(2)}, u32[]{:S(2)}) collective-permute-start(f32[8192]{0:T(1024)S(1)} %add.176), channel_id=1, source_target_pairs={{0,2},{1,3},{2,0},{3,1},{4,6},{5,7},{6,4},{7,5},{8,10},{9,11},{10,... | collective-permute-start | bytes 98312 | tf_op jit(solution)/shard_map/ppermute | solution.py:58
  45.5 3.9 %collective-permute-start.2 = (f32[8192]{0:T(1024)S(1)}, f32[8192]{0:T(1024)S(1)}, u32[]{:S(2)}, u32[]{:S(2)}) collective-permute-start(f32[8192]{0:T(1024)S(1)} %add.177), channel_id=1, source_target_pairs={{0,4},{1,5},{2,6},{3,7},{4,0},{5,1},{6,2},{7,3},{8,12},{9,13},{10,... | collective-permute-start | bytes 98312 | tf_op jit(solution)/shard_map/ppermute | solution.py:58
  49.4 40.9 %collective-permute-start.3 = (f32[8192]{0:T(1024)S(1)}, f32[8192]{0:T(1024)S(1)}, u32[]{:S(2)}, u32[]{:S(2)}) collective-permute-start(f32[8192]{0:T(1024)S(1)} %add.178), channel_id=1, source_target_pairs={{0,8},{1,9},{2,10},{3,11},{4,12},{5,13},{6,14},{7,15},{8,0},{9,1},... | collective-permute-start | bytes 98312 | tf_op jit(solution)/shard_map/ppermute | solution.py:58
  90.3 21.7 %collective-permute-start.4 = (f32[8192]{0:T(1024)S(1)}, f32[8192]{0:T(1024)S(1)}, u32[]{:S(2)}, u32[]{:S(2)}) collective-permute-start(f32[8192]{0:T(1024)S(1)} %add.179), channel_id=1, source_target_pairs={{0,16},{1,17},{2,18},{3,19},{4,20},{5,21},{6,22},{7,23},{8,24},{9,... | collective-permute-start | bytes 98312 | tf_op jit(solution)/shard_map/ppermute | solution.py:58
  91.2 24.8 %copy-start.1 = (bf16[256,8192]{1,0:T(8,128)(2,1)S(1)}, bf16[256,8192]{1,0:T(8,128)(2,1)}, u32[]{:S(2)}) copy-start(bf16[256,8192]{1,0:T(8,128)(2,1)} %param.10) | copy-start | bytes 12582916
  115.4 47.3 %copy-start.4 = (f32[256]{0:T(256)S(1)}, f32[256]{0:T(256)}, u32[]{:S(2)}) copy-start(f32[256]{0:T(256)} %param.14) | copy-start | bytes 3076
  247.2 44.8 %copy-start.5 = (f32[256]{0:T(256)}, f32[256]{0:T(256)S(1)}, u32[]{:S(2)}) copy-start(f32[256]{0:T(256)S(1)} %scatter_custom_fusion.1) | copy-start | bytes 3076
